TPU v7x, 128 devices: a whole 4x4x4 slice. The times are simulated.
128 devices in a mesh: ocn: 8 (over z, core), lon: 16 (over y, x).
Axes of the slice: x: 4, y: 4, z: 4, core: 2. Of those that a mesh axis runs over, the one named last changes fastest.
Arguments:
- ocean_state: bfloat16 [4, 12288, 128], P(None, ('ocn', 'lon')), may hold values from -6 to 6
- ice_cover: bfloat16 [12288, 128], P(('ocn', 'lon')), may hold values from 0 to 1
- ice_temp: bfloat16 [12288, 128], P(('ocn', 'lon')), may hold values from -6 to 6
- sea_mask: int32 [12288, 128], P(('ocn', 'lon')), may hold values from 0 to 1
- remap_tiles: bfloat16 [128, 640, 128, 128], P(('ocn', 'lon')), may hold values from 0 to 0.015625
- source_tile: int32 [128, 128, 5], P(('ocn', 'lon')), may hold values from 0 to 95
- send_block: int32 [128, 128, 5], P(('ocn', 'lon')), may hold values from -1 to 49, as said below
- recv_block: int32 [128, 128, 5], P(('ocn', 'lon')), may hold values from -1 to 49, as said below
- atm_state: float32 [4, 6400, 128], P(None, ('ocn', 'lon')), may hold values from -6 to 6
Outputs:
- ocean_fluxes: float32 [6, 12288, 128], P(None, ('ocn', 'lon'))
- atm_fluxes: float32 [6, 6400, 128], P(None, ('ocn', 'lon'))
Inputs may be any that keep to these rules, and one draw needn't show every extreme that they name: `send_block`: -1 marks an empty slot; every slot from a device to itself is filled. recv_block[e, s, c] equals send_block[s, e, c].
All inputs are finite; a program needn't handle non-finite values.
Results may differ from a plain program's by a relative error of at most 0.0019.
Values may be sent and summed in bfloat16 or wider, within the bound.
A program may use at most 64 MiB of HBM per device.

v0:
```python
import jax
import jax.numpy as jnp
from jax import lax
from jax.experimental import pallas as pl
from jax.experimental.pallas import tpu as pltpu
from jax.sharding import PartitionSpec as P

MESH = pl.DeviceIdType.MESH
ABP = 56
EARLY = 3
BACK_NEAR = True
LAG = 8


def exchange_kernel(dims, ocean, ice, ice_t, sea, tiles, src, snd, rcv, atm, ocean_out, atm_out,
                    ocean_v, ice_v, icet_v, sea_v, tiles_v, src_s, rcv_s, src_v, snd_v, rcv_v, atm_v,
                    stk, send1, recv1, send2, recv2, gath, ftab, terms, summed, in_sem, tile_sem, ssem1, rsem1, ssem2, rsem2):
    n_ocn, n_lon, cap, ob, ab, nz, ny, nx = dims
    core_n = n_ocn // nz
    f32, bf16 = jnp.float32, jnp.bfloat16
    o0, l0 = lax.axis_index("ocn"), lax.axis_index("lon")
    me = o0 * n_lon + l0
    z0, c0 = o0 // core_n, lax.rem(o0, core_n)
    y0, x0 = l0 // nx, lax.rem(l0, nx)
    half = n_lon // 2
    wave_slots = n_lon * cap
    peers = n_ocn * n_lon

    def wave_offset(w):
        i = w // core_n
        dz = lax.rem(i + 2, 4) + (i // 2) * (5 - 2 * i)
        return dz, core_n - 1 - lax.rem(w, core_n)

    def wave_to(w, near=False):
        w = n_ocn - 1 - w if near else w
        dz, dc = wave_offset(w)
        return lax.rem(z0 + dz, nz) * core_n + lax.rem(c0 + dc, core_n)

    def wave_from(w, near=False):
        w = n_ocn - 1 - w if near else w
        dz, dc = wave_offset(w)
        return lax.rem(z0 - dz + nz, nz) * core_n + lax.rem(c0 - dc + core_n, core_n)

    def lon_to(i):
        dy, dx = ny - 1 - i // nx, nx - 1 - lax.rem(i, nx)
        return lax.rem(y0 + dy, ny) * nx + lax.rem(x0 + dx, nx)

    small = [(ocean, ocean_v), (ice, ice_v), (ice_t, icet_v), (sea, sea_v), (src, src_s)]
    later = [(rcv, rcv_s), (src, src_v), (snd, snd_v), (rcv, rcv_v), (atm, atm_v.at[pl.ds(0, 4 * ab)])]
    copies = [pltpu.make_async_copy(a, b, in_sem.at[i]) for i, (a, b) in enumerate(small + later)]
    for c in copies[: len(small)]:
        c.start()

    def tile_copy(w):
        rows = pl.ds(wave_to(w) * wave_slots, wave_slots)
        return pltpu.make_async_copy(tiles.at[rows], tiles_v.at[rows], tile_sem.at[w])

    def start_tiles(w, _):
        tile_copy(w).start()
        return 0

    lax.fori_loop(0, n_ocn, start_tiles, 0)
    for c in copies[len(small):]:
        c.start()

    recv1[:, 32:40, :] = jnp.zeros((peers, 8, 128), bf16)

    barrier = pltpu.get_barrier_semaphore()

    def greet(k, _):
        o = wave_to(k // n_lon)
        l = lon_to(lax.rem(k, n_lon))

        @pl.when(k != peers - 1)
        def _():
            pl.semaphore_signal(barrier, inc=1, device_id=(o, l), device_id_type=MESH)

        return 0

    lax.fori_loop(0, peers, greet, 0)

    for c in copies[: len(small)]:
        c.wait()
    sea_f = sea_v[...].astype(f32)
    for f in range(4):
        stk[:, f, :] = ocean_v[f].astype(f32) * sea_f
    stk[:, 4, :] = ice_v[...].astype(f32) * sea_f
    stk[:, 5, :] = icet_v[...].astype(f32) * sea_f
    stk[:, 6, :] = sea_f
    stk[:, 7, :] = jnp.zeros((ob, 128), f32)

    sub = lax.broadcasted_iota(jnp.int32, (8, 128), 0)

    def forward(w):
        o = wave_to(w)

        def part(h, _):
            for i in range(half):
                e = o * n_lon + lon_to(h * half + i)
                rows = [
                    jnp.dot(
                        stk[src_s[c, 0, e]].astype(bf16), tiles_v[e * cap + c], preferred_element_type=f32
                    )
                    for c in range(cap)
                ]
                for c in range(4):
                    rows[c] = jnp.where(sub == 7, pltpu.roll(rows[4], 7 - c, 0), rows[c])
                rows[4] = pltpu.roll(rows[4], 4, 0)
                for c in range(cap):
                    send1[e, 8 * c : 8 * c + 8, :] = rows[c].astype(bf16)
            return 0

        tile_copy(w).wait()
        lax.fori_loop(0, 2, part, 0)

    def push(w, buf, out, ssem, rsem, rows, near=False):
        o = wave_to(w, near)
        last = 0 if near else n_ocn - 1

        def one(j, _):
            l = lon_to(j)
            e = o * n_lon + l

            @pl.when(w * n_lon + j != last * n_lon + n_lon - 1)
            def _():
                pltpu.make_async_remote_copy(
                    buf.at[e, pl.ds(0, rows)], out.at[me, pl.ds(0, rows)], ssem, rsem.at[w], device_id=(o, l), device_id_type=MESH
                ).start()

            return 0

        lax.fori_loop(0, n_lon, one, 0)

    def forward_early(w, _):
        forward(w)
        return 0

    def push_early(w, _):
        push(w, send1, recv1, ssem1, rsem1, 36)
        return 0

    def forward_step(w, _):
        forward(w)
        push(w, send1, recv1, ssem1, rsem1, 36)
        return 0

    lax.fori_loop(0, EARLY, forward_early, 0)
    pl.semaphore_wait(barrier, peers - 1)
    lax.fori_loop(0, EARLY, push_early, 0)
    lax.fori_loop(EARLY, n_ocn, forward_step, 0)
    recv1[me] = send1[me]

    for c in copies[len(small):]:
        c.wait()

    def padded(table):
        return jnp.concatenate([table, jnp.zeros((8 - cap, peers), f32)], 0).astype(bf16)

    rcv_f = rcv_v[:, 0, :].astype(f32)
    rcv_table = padded(jnp.where(rcv_f < 0, -1000.0, rcv_f))
    src_table = padded(jnp.where(snd_v[:, 0, :] < 0, -1000.0, src_v[:, 0, :].astype(f32)))

    def onehot(table, count, o, width=None):
        rep = 1 if width is None else 8
        k = wave_slots * rep
        lanes = lax.broadcasted_iota(jnp.int32, (peers, k), 1)
        first = (lax.broadcasted_iota(jnp.int32, (peers, k), 0) - o * n_lon) * (rep * cap)
        spread = jnp.where((lanes >= first) & (lanes < first + rep * cap), 1.0, 0.0).astype(bf16)
        entries = jnp.dot(table, spread, preferred_element_type=f32)
        place = lax.rem(lax.broadcasted_iota(jnp.int32, (8, k), 1), rep * cap)
        slot = place // rep
        if width is not None:
            slot = jnp.where(lax.rem(place, rep) == 7, cap - 1, slot)
        chosen = slot == lax.broadcasted_iota(jnp.int32, (8, k), 0)
        code = jnp.sum(jnp.where(chosen, entries, 0.0), axis=0, keepdims=True)
        if width is not None:
            place = place[:1]
            field = jnp.where(lax.rem(place, rep) == 7, place // rep, lax.rem(place, rep))
            field = jnp.where(place >= rep * (cap - 1), place - (rep * (cap - 1) - 4), field)
            code = code + field.astype(f32) * float(width)
        rows = lax.broadcasted_iota(jnp.int32, (count, 1), 0).astype(f32)
        return jnp.where(rows == code, 1.0, 0.0).astype(bf16)

    def wave_wait(buf, rsem, w, rows, near=False):
        last = 0 if near else n_ocn - 1

        @pl.when(w == last)
        def _():
            part = buf.at[pl.ds(0, n_lon - 1), pl.ds(0, rows)]
            pltpu.make_async_copy(part, part, rsem.at[w]).wait()

        @pl.when(w != last)
        def _():
            part = buf.at[pl.ds(0, n_lon), pl.ds(0, rows)]
            pltpu.make_async_copy(part, part, rsem.at[w]).wait()

    gath[...] = jnp.zeros_like(gath)

    def gather_step(w, _):
        o = wave_from(w)
        hot = onehot(rcv_table, 7 * ABP, o, ABP)
        wave_wait(recv1, rsem1, w, 36)
        part = recv1[pl.ds(o * n_lon, n_lon)].reshape(n_lon * 8 * cap, 128)
        gath[...] += jnp.dot(hot, part, preferred_element_type=f32)
        return 0

    lax.fori_loop(0, n_ocn, gather_step, 0)

    atm_v[pl.ds(4 * ab, 4 * (ABP - ab)), :] = jnp.zeros((4 * (ABP - ab), 128), f32)
    g = [gath[f * ABP : (f + 1) * ABP, :] for f in range(7)]
    a = [atm_v[pl.ds(f, ABP, stride=4), :] for f in range(4)]
    inverse = 1.0 / jnp.maximum(g[6], 0.1)
    surface_temp, current_u, current_v, salinity, ice_frac, ice_surface = [g[f] * inverse for f in range(6)]
    slip_east = a[0] - current_u
    slip_north = a[1] - current_v
    wind_speed = jnp.sqrt(slip_east * slip_east + slip_north * slip_north + 0.25)
    open_water = 1.0 - ice_frac
    saturation = 0.5 * jnp.exp(0.2 * surface_temp) * (1.0 - 0.05 * salinity)
    evaporation = 0.3 * open_water * wind_speed * (saturation - a[3])
    heat = (
        0.3 * wind_speed * (open_water * (surface_temp - a[2]) + ice_frac * (ice_surface - a[2]))
        + 2.5 * evaporation
    )
    fluxes = [
        0.5 * open_water * wind_speed * slip_east,
        0.5 * open_water * wind_speed * slip_north,
        0.8 * ice_frac * wind_speed * slip_east,
        0.8 * ice_frac * wind_speed * slip_north,
        heat,
        evaporation,
    ]
    zero = jnp.zeros((ABP, 128), f32)
    for v in range(4):
        ftab[v * (ABP + 8)] = jnp.zeros((8, 128), f32)
        for r in range(8):
            if v == 0:
                value = fluxes[r] if r < 6 else zero
            else:
                value = fluxes[2 * (v - 1) + r - 6] if r >= 6 else zero
            ftab[v * (ABP + 8) + 1 : v * (ABP + 8) + 1 + ABP, r, :] = value
    for f in range(6):
        atm_out[f] = fluxes[f][:ab]

    def pack(w):
        o = wave_to(w, BACK_NEAR)

        def part(h, _):
            for i in range(half):
                e = o * n_lon + lon_to(h * half + i)

                def row(v, c):
                    return ftab[rcv_s[c, 0, e] + (v * (ABP + 8) + 1)]

                for c in range(4):
                    value = row(0, c) + row(c + 1, 4) if c < 3 else row(0, c)
                    send2[e, 8 * c : 8 * c + 8, :] = value.astype(bf16)
            return 0

        lax.fori_loop(0, 2, part, 0)

    def back_step(w, _):
        pack(w)
        push(w, send2, recv2, ssem2, rsem2, 32, BACK_NEAR)

        @pl.when(w == (0 if BACK_NEAR else n_ocn - 1))
        def _():
            recv2[me] = send2[me]

        return 0

    lax.fori_loop(0, LAG, back_step, 0)

    summed[...] = jnp.zeros_like(summed)

    def ocean_step(w, _):
        if LAG < n_ocn:

            @pl.when(w < n_ocn - LAG)
            def _():
                back_step(w + LAG, 0)

        o = wave_from(w, BACK_NEAR)
        hot = onehot(src_table, ob, o)
        wave_wait(recv2, rsem2, w, 32, BACK_NEAR)

        def part_step(p, _):
            for i in range(half):
                q = p * half + i
                s = o * n_lon + q
                block = recv2[s].astype(f32)
                v = [block[8 * c : 8 * c + 8] for c in range(4)]
                last = jnp.where(
                    sub < 2,
                    pltpu.roll(v[0], 2, 0),
                    jnp.where(sub < 4, pltpu.roll(v[1], 4, 0), pltpu.roll(v[2], 6, 0)),
                )
                for c, rows in enumerate(v + [last]):
                    lhs = jnp.where(sub == 6, 1.0, jnp.where(sub == 7, 0.0, rows)).astype(bf16)
                    term = lax.dot_general(
                        lhs, tiles_v[s * cap + c], (((1,), (1,)), ((), ())), preferred_element_type=f32
                    )
                    terms[pl.ds(q * cap + c, 8, stride=wave_slots), :] = term
            return 0

        lax.fori_loop(0, 2, part_step, 0)
        for f in range(7):
            term = terms[f * wave_slots : (f + 1) * wave_slots, :]
            hi = term.astype(bf16)
            lo = (term - hi.astype(f32)).astype(bf16)
            both = jnp.dot(hot, jnp.concatenate([hi, lo], 1), preferred_element_type=f32)
            summed[f * ob : (f + 1) * ob, :] += both[:, :128] + both[:, 128:]
        return 0

    lax.fori_loop(0, n_ocn, ocean_step, 0)
    scale = sea_v[...].astype(f32) / jnp.maximum(summed[6 * ob : 7 * ob, :], 0.1)
    for f in range(6):
        ocean_out[f] = summed[f * ob : (f + 1) * ob, :] * scale
    for buf, ssem, rows in ((send1, ssem1, 36), (send2, ssem2, 32)):
        part = buf.at[pl.ds(0, peers - 1), pl.ds(0, rows)]
        pltpu.make_async_copy(part, part, ssem).wait()


def finish_kernel(ocean_in, atm_in, ocean_out, atm_out, ocean_v, atm_v, in_sem, out_sem):
    reads = [
        pltpu.make_async_copy(ocean_in, ocean_v, in_sem.at[0]),
        pltpu.make_async_copy(atm_in, atm_v, in_sem.at[1]),
    ]
    writes = [
        pltpu.make_async_copy(ocean_v, ocean_out, out_sem.at[0]),
        pltpu.make_async_copy(atm_v, atm_out, out_sem.at[1]),
    ]
    for c in reads:
        c.start()
    for r, c in zip(reads, writes):
        r.wait()
        c.start()
    for c in writes:
        c.wait()


def shards(ocean_state, ice_cover, ice_temp, sea_mask, remap_tiles, source_tile, send_block, recv_block, atm_state):
    n_ocn, n_lon = lax.axis_size("ocn"), lax.axis_size("lon")
    peers = n_ocn * n_lon
    ob, ab = sea_mask.shape[0], atm_state.shape[1]
    slots = remap_tiles.shape[1]
    cap = slots // peers
    dims = (n_ocn, n_lon, cap, ob, ab, 4, 4, 4)
    f32, bf16, i32 = jnp.float32, jnp.bfloat16, jnp.int32

    def table(x):
        return x.transpose(2, 0, 1)

    hbm_spec = pl.BlockSpec(memory_space=pltpu.HBM)
    dma = pltpu.SemaphoreType.DMA

    def body(*refs):
        exchange_kernel(dims, *refs)

    ocean_sums, fluxes = pl.pallas_call(
        body,
        out_shape=(
            jax.ShapeDtypeStruct((6, ob, 128), f32),
            jax.ShapeDtypeStruct((6, ab, 128), f32),
        ),
        in_specs=[hbm_spec] * 9,
        out_specs=(pl.BlockSpec(memory_space=pltpu.VMEM),) * 2,
        scratch_shapes=[
            pltpu.VMEM((4, ob, 128), bf16),
            pltpu.VMEM((ob, 128), bf16),
            pltpu.VMEM((ob, 128), bf16),
            pltpu.VMEM((ob, 128), i32),
            pltpu.VMEM((slots, 128, 128), bf16),
            pltpu.SMEM((cap, 1, peers), i32),
            pltpu.SMEM((cap, 1, peers), i32),
            pltpu.VMEM((cap, 1, peers), i32),
            pltpu.VMEM((cap, 1, peers), i32),
            pltpu.VMEM((cap, 1, peers), i32),
            pltpu.VMEM((4 * ABP, 128), f32),
            pltpu.VMEM((ob, 8, 128), f32),
            pltpu.VMEM((peers, 8 * cap, 128), bf16),
            pltpu.VMEM((peers, 8 * cap, 128), bf16),
            pltpu.VMEM((peers, 32, 128), bf16),
            pltpu.VMEM((peers, 32, 128), bf16),
            pltpu.VMEM((7 * ABP, 128), f32),
            pltpu.VMEM((4 * (ABP + 8), 8, 128), f32),
            pltpu.VMEM((8 * n_lon * cap, 128), f32),
            pltpu.VMEM((7 * ob, 128), f32),
            dma((10,)),
            dma((n_ocn,)),
            dma,
            dma((n_ocn,)),
            dma,
            dma((n_ocn,)),
        ],
        compiler_params=pltpu.CompilerParams(
            collective_id=0, has_side_effects=True, vmem_limit_bytes=66300000
        ),
        name="exchange",
    )(
        ocean_state,
        ice_cover,
        ice_temp,
        sea_mask,
        remap_tiles[0],
        table(source_tile),
        table(send_block),
        table(recv_block),
        atm_state.transpose(1, 0, 2).reshape(4 * ab, 128),
    )
    return pl.pallas_call(
        finish_kernel,
        out_shape=(
            jax.ShapeDtypeStruct((6, ob, 128), f32),
            jax.ShapeDtypeStruct((6, ab, 128), f32),
        ),
        in_specs=[hbm_spec] * 2,
        out_specs=(hbm_spec,) * 2,
        scratch_shapes=[pltpu.VMEM((6, ob, 128), f32), pltpu.VMEM((6, ab, 128), f32), dma((2,)), dma((2,))],
        name="finish",
    )(ocean_sums, fluxes)


def solution(mesh):
    in_specs = (
        P(None, ("ocn", "lon"), None),
        P(("ocn", "lon"), None),
        P(("ocn", "lon"), None),
        P(("ocn", "lon"), None),
        P(("ocn", "lon"), None, None, None),
        P(("ocn", "lon"), None, None),
        P(("ocn", "lon"), None, None),
        P(("ocn", "lon"), None, None),
        P(None, ("ocn", "lon"), None),
    )
    out_specs = (P(None, ("ocn", "lon"), None), P(None, ("ocn", "lon"), None))
    return jax.shard_map(shards, mesh=mesh, in_specs=in_specs, out_specs=out_specs, check_vma=False)
```

profile of v0, /device:TPU:1, one launch (start us, length us, event | category | flops | bytes accessed | tf_op | source)
XLA Modules:
  0.0 62.2 jit_solution(10647388604927141370)
XLA Ops:
  0.6 59.8 %exchange.1 = (f32[6,96,128]{2,1,0:T(8,128)}, f32[6,50,128]{2,1,0:T(8,128)}) custom-call(bf16[4,96,128]{2,1,0:T(8,128)(2,1)} %refs_0_.1, bf16[96,128]{1,0:T(8,128)(2,1)} %refs_1_.1, bf16[96,128]{1,0:T(8,128)(2,1)} %refs_2_.1, s32[96,128]{1,0:T(8,128)} %refs_3_.1, bf16[640,128,128]{2,1,0:T(8,128)(2,1)} %bitcast.7, s32[5,1,128]{2,1,0:T(1,128)} %bitcast.9, ...), custom_call_target="tpu_custom_call" | custom-call | tf_op jit(solution)/shard_map/exchange/pallas_call | solution.py:359
  60.4 1.8 %finish.1 = (f32[6,96,128]{2,1,0:T(8,128)}, f32[6,50,128]{2,1,0:T(8,128)}) custom-call(f32[6,96,128]{2,1,0:T(8,128)} %get-tuple-element.4.ocean_in, f32[6,50,128]{2,1,0:T(8,128)} %get-tuple-element.5.atm_in), custom_call_target="tpu_custom_call" | custom-call | tf_op jit(solution)/shard_map/finish/pallas_call | solution.py:410
where the time goes:
time: 62.3 us; the launch traced here: 62.2 us
  Pallas kernels  61.5 us (99%)
  between operations  0.64 us (1%)
    pallas_call x1, Pallas kernels, shards(): pl.pallas_call(body, out_shape=(jax.ShapeDtypeStruct((6, ob, 128), f32),...  59.8 us
    pallas_call x1, Pallas kernels, shards(): pl.pallas_call(finish_kernel, out_shape=(jax.ShapeDtypeStruct((6, ob, 128...  1.76 us

commit v1 on v0

--- a/solution.py
+++ b/solution.py
@@ -7,9 +7,15 @@
 
 MESH = pl.DeviceIdType.MESH
 ABP = 56
-EARLY = 3
+EARLY = 2
 BACK_NEAR = True
+AHEAD = 2
 LAG = 8
+
+
+def slot_pairs(cap):
+    slots = [(0, c) for c in range(cap)] + [(1, c) for c in range(cap)]
+    return [(slots[i], slots[i + 1]) for i in range(0, 2 * cap, 2)]
 
 
 def exchange_kernel(dims, ocean, ice, ice_t, sea, tiles, src, snd, rcv, atm, ocean_out, atm_out,
@@ -55,11 +61,8 @@
         rows = pl.ds(wave_to(w) * wave_slots, wave_slots)
         return pltpu.make_async_copy(tiles.at[rows], tiles_v.at[rows], tile_sem.at[w])
 
-    def start_tiles(w, _):
+    for w in range(AHEAD):
         tile_copy(w).start()
-        return 0
-
-    lax.fori_loop(0, n_ocn, start_tiles, 0)
     for c in copies[len(small):]:
         c.start()
 
@@ -95,20 +98,30 @@
         o = wave_to(w)
 
         def part(h, _):
-            for i in range(half):
-                e = o * n_lon + lon_to(h * half + i)
-                rows = [
-                    jnp.dot(
-                        stk[src_s[c, 0, e]].astype(bf16), tiles_v[e * cap + c], preferred_element_type=f32
-                    )
-                    for c in range(cap)
-                ]
-                for c in range(4):
-                    rows[c] = jnp.where(sub == 7, pltpu.roll(rows[4], 7 - c, 0), rows[c])
-                rows[4] = pltpu.roll(rows[4], 4, 0)
-                for c in range(cap):
-                    send1[e, 8 * c : 8 * c + 8, :] = rows[c].astype(bf16)
+            for i in range(0, half, 2):
+                two = [o * n_lon + lon_to(h * half + i + d) for d in range(2)]
+
+                def remap(p, q):
+                    lhs = jnp.concatenate([stk[src_s[c, 0, two[d]]] for d, c in (p, q)], 0).astype(bf16)
+                    rhs = jnp.concatenate([tiles_v[two[d] * cap + c] for d, c in (p, q)], 1)
+                    both = jnp.dot(lhs, rhs, preferred_element_type=f32)
+                    rows[p] = both[:8, :128]
+                    rows[q] = both[8:, 128:]
+
+                rows = {}
+                for p, q in slot_pairs(cap):
+                    remap(p, q)
+                for d in range(2):
+                    last = rows[d, cap - 1]
+                    for c in range(cap - 1):
+                        value = jnp.where(sub == 7, pltpu.roll(last, 7 - c, 0), rows[d, c])
+                        send1[two[d], 8 * c : 8 * c + 8, :] = value.astype(bf16)
+                    send1[two[d], 32:40, :] = pltpu.roll(last, 4, 0).astype(bf16)
             return 0
+
+        @pl.when(w < n_ocn - AHEAD)
+        def _():
+            tile_copy(w + AHEAD).start()
 
         tile_copy(w).wait()
         lax.fori_loop(0, 2, part, 0)
@@ -260,7 +273,7 @@
 
     def back_step(w, _):
         pack(w)
-        push(w, send2, recv2, ssem2, rsem2, 32, BACK_NEAR)
+        push(w, send2, recv2, ssem2, rsem2, 30, BACK_NEAR)
 
         @pl.when(w == (0 if BACK_NEAR else n_ocn - 1))
         def _():
@@ -281,25 +294,32 @@
 
         o = wave_from(w, BACK_NEAR)
         hot = onehot(src_table, ob, o)
-        wave_wait(recv2, rsem2, w, 32, BACK_NEAR)
+        wave_wait(recv2, rsem2, w, 30, BACK_NEAR)
 
         def part_step(p, _):
-            for i in range(half):
-                q = p * half + i
-                s = o * n_lon + q
-                block = recv2[s].astype(f32)
-                v = [block[8 * c : 8 * c + 8] for c in range(4)]
-                last = jnp.where(
-                    sub < 2,
-                    pltpu.roll(v[0], 2, 0),
-                    jnp.where(sub < 4, pltpu.roll(v[1], 4, 0), pltpu.roll(v[2], 6, 0)),
-                )
-                for c, rows in enumerate(v + [last]):
-                    lhs = jnp.where(sub == 6, 1.0, jnp.where(sub == 7, 0.0, rows)).astype(bf16)
-                    term = lax.dot_general(
-                        lhs, tiles_v[s * cap + c], (((1,), (1,)), ((), ())), preferred_element_type=f32
+            for i in range(0, half, 2):
+                place = [p * half + i + d for d in range(2)]
+                base = [(o * n_lon + place[d]) * cap for d in range(2)]
+                lhs = {}
+                for d in range(2):
+                    block = recv2[o * n_lon + place[d]].astype(f32)
+                    v = [block[8 * c : 8 * c + 8] for c in range(4)]
+                    last = jnp.where(
+                        sub < 2,
+                        pltpu.roll(v[0], 2, 0),
+                        jnp.where(sub < 4, pltpu.roll(v[1], 4, 0), pltpu.roll(v[2], 6, 0)),
                     )
-                    terms[pl.ds(q * cap + c, 8, stride=wave_slots), :] = term
+                    for c, rows in enumerate(v + [last]):
+                        lhs[d, c] = jnp.where(sub == 6, 1.0, jnp.where(sub == 7, 0.0, rows))
+                for x, y in slot_pairs(cap):
+                    both = lax.dot_general(
+                        jnp.concatenate([lhs[x], lhs[y]], 0).astype(bf16),
+                        jnp.concatenate([tiles_v[base[d] + c] for d, c in (x, y)], 0),
+                        (((1,), (1,)), ((), ())),
+                        preferred_element_type=f32,
+                    )
+                    for (d, c), term in ((x, both[:8, :128]), (y, both[8:, 128:])):
+                        terms[pl.ds(place[d] * cap + c, 8, stride=wave_slots), :] = term
             return 0
 
         lax.fori_loop(0, 2, part_step, 0)
@@ -315,7 +335,7 @@
     scale = sea_v[...].astype(f32) / jnp.maximum(summed[6 * ob : 7 * ob, :], 0.1)
     for f in range(6):
         ocean_out[f] = summed[f * ob : (f + 1) * ob, :] * scale
-    for buf, ssem, rows in ((send1, ssem1, 36), (send2, ssem2, 32)):
+    for buf, ssem, rows in ((send1, ssem1, 36), (send2, ssem2, 30)):
         part = buf.at[pl.ds(0, peers - 1), pl.ds(0, rows)]
         pltpu.make_async_copy(part, part, ssem).wait()
 

time: 62.3 us -> 59.8 us (0.960)
  Pallas kernels: 61.5 us -> 59 us
    pallas_call x1, Pallas kernels: 59.8 us -> 57.2 us  [shards(): pl.pallas_call(body, out_shape=(jax.ShapeDtypeStruct((6, ob, 128), f32),...]
where the time goes in v1:
time: 59.8 us; the launch traced here: 59.6 us
  Pallas kernels  59 us (99%)
  between operations  0.64 us (1%)
    pallas_call x1, Pallas kernels, shards(): pl.pallas_call(body, out_shape=(jax.ShapeDtypeStruct((6, ob, 128), f32),...  57.2 us
    pallas_call x1, Pallas kernels, shards(): pl.pallas_call(finish_kernel, out_shape=(jax.ShapeDtypeStruct((6, ob, 128...  1.76 us

profile of v1, /device:TPU:1, one launch (start us, length us, event | category | flops | bytes accessed | tf_op | source)
XLA Modules:
  0.0 59.6 jit_solution(1043785536024923894)
XLA Ops:
  0.6 57.2 %exchange.1 = (f32[6,96,128]{2,1,0:T(8,128)}, f32[6,50,128]{2,1,0:T(8,128)}) custom-call(bf16[4,96,128]{2,1,0:T(8,128)(2,1)} %refs_0_.1, bf16[96,128]{1,0:T(8,128)(2,1)} %refs_1_.1, bf16[96,128]{1,0:T(8,128)(2,1)} %refs_2_.1, s32[96,128]{1,0:T(8,128)} %refs_3_.1, bf16[640,128,128]{2,1,0:T(8,128)(2,1)} %bitcast.7, s32[5,1,128]{2,1,0:T(1,128)} %bitcast.9, ...), custom_call_target="tpu_custom_call" | custom-call | tf_op jit(solution)/shard_map/exchange/pallas_call | solution.py:379
  57.9 1.8 %finish.1 = (f32[6,96,128]{2,1,0:T(8,128)}, f32[6,50,128]{2,1,0:T(8,128)}) custom-call(f32[6,96,128]{2,1,0:T(8,128)} %get-tuple-element.4.ocean_in, f32[6,50,128]{2,1,0:T(8,128)} %get-tuple-element.5.atm_in), custom_call_target="tpu_custom_call" | custom-call | tf_op jit(solution)/shard_map/finish/pallas_call | solution.py:430

commit v2 on v1

--- a/solution.py
+++ b/solution.py
@@ -7,9 +7,9 @@
 
 MESH = pl.DeviceIdType.MESH
 ABP = 56
-EARLY = 2
+EARLY = 3
 BACK_NEAR = True
-AHEAD = 2
+AHEAD = 3
 LAG = 8
 
 
@@ -34,7 +34,7 @@
 
     def wave_offset(w):
         i = w // core_n
-        dz = lax.rem(i + 2, 4) + (i // 2) * (5 - 2 * i)
+        dz = 3 - i
         return dz, core_n - 1 - lax.rem(w, core_n)
 
     def wave_to(w, near=False):
@@ -208,6 +208,8 @@
             pltpu.make_async_copy(part, part, rsem.at[w]).wait()
 
     gath[...] = jnp.zeros_like(gath)
+    ftab[...] = jnp.zeros_like(ftab)
+    summed[...] = jnp.zeros_like(summed)
 
     def gather_step(w, _):
         o = wave_from(w)
@@ -242,15 +244,10 @@
         heat,
         evaporation,
     ]
-    zero = jnp.zeros((ABP, 128), f32)
-    for v in range(4):
-        ftab[v * (ABP + 8)] = jnp.zeros((8, 128), f32)
-        for r in range(8):
-            if v == 0:
-                value = fluxes[r] if r < 6 else zero
-            else:
-                value = fluxes[2 * (v - 1) + r - 6] if r >= 6 else zero
-            ftab[v * (ABP + 8) + 1 : v * (ABP + 8) + 1 + ABP, r, :] = value
+    for f in range(6):
+        v = 1 + f // 2
+        ftab[1 : 1 + ABP, f, :] = fluxes[f]
+        ftab[v * (ABP + 8) + 1 : v * (ABP + 8) + 1 + ABP, 6 + f % 2, :] = fluxes[f]
     for f in range(6):
         atm_out[f] = fluxes[f][:ab]
 
@@ -283,7 +280,6 @@
 
     lax.fori_loop(0, LAG, back_step, 0)
 
-    summed[...] = jnp.zeros_like(summed)
 
     def ocean_step(w, _):
         if LAG < n_ocn:

time: 59.8 us -> 58 us (0.970)
  Pallas kernels: 59 us -> 57.6 us
    pallas_call x1, Pallas kernels: 57.2 us -> 55.8 us  [shards(): pl.pallas_call(body, out_shape=(jax.ShapeDtypeStruct((6, ob, 128), f32),...]
where the time goes in v2:
time: 58 us; the launch traced here: 58.2 us
  Pallas kernels  57.6 us (99%)
  between operations  0.64 us (1%)
    pallas_call x1, Pallas kernels, shards(): pl.pallas_call(body, out_shape=(jax.ShapeDtypeStruct((6, ob, 128), f32),...  55.8 us
    pallas_call x1, Pallas kernels, shards(): pl.pallas_call(finish_kernel, out_shape=(jax.ShapeDtypeStruct((6, ob, 128...  1.76 us

profile of v2, /device:TPU:1, one launch (start us, length us, event | category | flops | bytes accessed | tf_op | source)
XLA Modules:
  0.0 58.2 jit_solution(15568622621696034152)
XLA Ops:
  0.6 55.8 %exchange.1 = (f32[6,96,128]{2,1,0:T(8,128)}, f32[6,50,128]{2,1,0:T(8,128)}) custom-call(bf16[4,96,128]{2,1,0:T(8,128)(2,1)} %refs_0_.1, bf16[96,128]{1,0:T(8,128)(2,1)} %refs_1_.1, bf16[96,128]{1,0:T(8,128)(2,1)} %refs_2_.1, s32[96,128]{1,0:T(8,128)} %refs_3_.1, bf16[640,128,128]{2,1,0:T(8,128)(2,1)} %bitcast.7, s32[5,1,128]{2,1,0:T(1,128)} %bitcast.9, ...), custom_call_target="tpu_custom_call" | custom-call | tf_op jit(solution)/shard_map/exchange/pallas_call | solution.py:375
  56.4 1.8 %finish.1 = (f32[6,96,128]{2,1,0:T(8,128)}, f32[6,50,128]{2,1,0:T(8,128)}) custom-call(f32[6,96,128]{2,1,0:T(8,128)} %get-tuple-element.4.ocean_in, f32[6,50,128]{2,1,0:T(8,128)} %get-tuple-element.5.atm_in), custom_call_target="tpu_custom_call" | custom-call | tf_op jit(solution)/shard_map/finish/pallas_call | solution.py:426

commit v3 on v2

--- a/solution.py
+++ b/solution.py
@@ -7,7 +7,7 @@
 
 MESH = pl.DeviceIdType.MESH
 ABP = 56
-EARLY = 3
+EARLY = 4
 BACK_NEAR = True
 AHEAD = 3
 LAG = 8

time: 58 us -> 56.7 us (0.978)
  Pallas kernels: 57.6 us -> 56 us
    pallas_call x1, Pallas kernels: 55.8 us -> 54.2 us  [shards(): pl.pallas_call(body, out_shape=(jax.ShapeDtypeStruct((6, ob, 128), f32),...]
where the time goes in v3:
time: 56.7 us; the launch traced here: 56.6 us
  Pallas kernels  56 us (99%)
  between operations  0.64 us (1%)
    pallas_call x1, Pallas kernels, shards(): pl.pallas_call(body, out_shape=(jax.ShapeDtypeStruct((6, ob, 128), f32),...  54.2 us
    pallas_call x1, Pallas kernels, shards(): pl.pallas_call(finish_kernel, out_shape=(jax.ShapeDtypeStruct((6, ob, 128...  1.76 us

profile of v3, /device:TPU:1, one launch (start us, length us, event | category | flops | bytes accessed | tf_op | source)
XLA Modules:
  0.0 56.6 jit_solution(7155354187889916919)
XLA Ops:
  0.6 54.2 %exchange.1 = (f32[6,96,128]{2,1,0:T(8,128)}, f32[6,50,128]{2,1,0:T(8,128)}) custom-call(bf16[4,96,128]{2,1,0:T(8,128)(2,1)} %refs_0_.1, bf16[96,128]{1,0:T(8,128)(2,1)} %refs_1_.1, bf16[96,128]{1,0:T(8,128)(2,1)} %refs_2_.1, s32[96,128]{1,0:T(8,128)} %refs_3_.1, bf16[640,128,128]{2,1,0:T(8,128)(2,1)} %bitcast.7, s32[5,1,128]{2,1,0:T(1,128)} %bitcast.9, ...), custom_call_target="tpu_custom_call" | custom-call | tf_op jit(solution)/shard_map/exchange/pallas_call | solution.py:375
  54.8 1.8 %finish.1 = (f32[6,96,128]{2,1,0:T(8,128)}, f32[6,50,128]{2,1,0:T(8,128)}) custom-call(f32[6,96,128]{2,1,0:T(8,128)} %get-tuple-element.4.ocean_in, f32[6,50,128]{2,1,0:T(8,128)} %get-tuple-element.5.atm_in), custom_call_target="tpu_custom_call" | custom-call | tf_op jit(solution)/shard_map/finish/pallas_call | solution.py:426
